TPU v7x, 512 devices: a whole 4x4x16 slice. The times are simulated.
512 devices in a mesh: seq: 128 (over x, z, core), head: 4 (over y).
Axes of the slice: x: 4, y: 4, z: 16, core: 2. Of those that a mesh axis runs over, the one named last changes fastest.
Arguments:
- values_in: bfloat16 [65536, 4096], P('seq', 'head'), may hold values from -6 to 6
- gate_in: bfloat16 [65536, 4096], P('seq', 'head'), may hold values from -6 to 6
- key_proj: bfloat16 [65536, 128], P('seq'), may hold values from -0.52734375 to 0.52734375
- query_proj: bfloat16 [65536, 128], P('seq'), may hold values from -6 to 6
- step_size: float32 [65536, 64], P('seq', 'head'), may hold values from 0.5 to 2
- log_decay: float32 [65536, 64], P('seq', 'head'), may hold values from -1.2 to 0
- skip_weight: float32 [64], P('head'), may hold values from 0.5 to 1.5
- norm_gain: float32 [4096], P('head'), may hold values from 0.5 to 1.5
- level_table: float32 [16, 64, 11], P(None, 'head'), may hold values from 0.25 to 2
- level_pick: int32 [65536], P('seq'), may hold values from 0 to 15
- doc_start: int32 [1024], P('seq'), may hold values 0 or 1
Outputs:
- layer_out: bfloat16 [65536, 4096], P('seq', 'head')
All inputs are finite; a program needn't handle non-finite values. No bound on the sum of `doc_start` on one device may be relied on, other than what follows from the above.
Results may differ from a plain program's by a relative error of at most 0.012.
Values may be sent and summed in bfloat16 or wider, within the bound.
A program may use at most 64 MiB of HBM per device.

v0:
```python
import math
import jax
import jax.numpy as jnp
from jax import lax
from jax.sharding import Mesh
from jax.sharding import PartitionSpec as P

H = 64
HEADDIM = 64
STRETCH = 64
SEQ = ("seq_0", "seq_1", "seq_2")
epsilon = 1e-06


def joined_along(pieces, dim):
    pieces = jnp.moveaxis(pieces, 0, dim)
    shape = pieces.shape
    return pieces.reshape(*shape[:dim], shape[dim] * shape[dim + 1], *shape[dim + 2 :])


def gather_in_order(array, axes, turns):
    pieces = array[None]
    for k in turns:
        pieces = lax.all_gather(pieces, axes[k], axis=0, tiled=True)
    current = [lax.axis_size(axes[k]) for k in reversed(turns)]
    pieces = pieces.reshape(*current, *array.shape)
    turned = sorted(range(len(turns)), key=lambda place: turns[len(turns) - 1 - place])
    return pieces.transpose(*turned, *range(len(turns), pieces.ndim)).reshape(-1, *array.shape)


def gathered_by_axis(array, axes, turns, dim):
    return joined_along(gather_in_order(array, axes, turns), dim)


def copy_for_each(array, axis):
    size = lax.axis_size(axis)
    return lax.all_to_all(
        jnp.broadcast_to(array[None], (size, *array.shape)), axis, 0, 0, tiled=True
    )


def over_copies(array, axis):
    everything = copy_for_each(array, axis)
    return jnp.sum(everything, axis=0)


def level_of_pairs(row_count, stretch_len, low_bits):
    blocks = jnp.arange(row_count, dtype=jnp.int32) // stretch_len
    differ = jnp.bitwise_xor(blocks[:, None], blocks[None, :])
    level_index = jnp.zeros((row_count, row_count), jnp.int32)
    for bit_index in range(low_bits):
        level_index = level_index + (differ >= 1 << bit_index).astype(jnp.int32)
    return level_index


def flip_pairs(tensor, bit_index):
    split_view = tensor.reshape(
        (tensor.shape[0] >> bit_index + 1, 2, 1 << bit_index) + tensor.shape[1:]
    )
    return split_view[:, ::-1].reshape(tensor.shape)


def local(
    values_in,
    gate_in,
    key_proj,
    query_proj,
    step_size,
    log_decay,
    skip_weight,
    norm_gain,
    level_table,
    level_pick,
    doc_start,
):
    tok_rows = values_in.shape[0]
    head_count = step_size.shape[1]
    head_width = HEADDIM
    state_width = key_proj.shape[1]
    per_span = doc_start.shape[0]
    low_bits = per_span.bit_length() - 1
    span_total = lax.axis_size(SEQ)
    span_bits = span_total.bit_length() - 1
    table_rows = level_table.shape[0]
    level_count = level_table.shape[2]
    one_hot = (level_pick[:, None] == jnp.arange(table_rows, dtype=jnp.int32)[None, :]).astype(
        jnp.float32
    )
    level_weight = jnp.dot(
        one_hot,
        level_table.reshape(table_rows, head_count * level_count),
        precision=lax.Precision.HIGHEST,
        preferred_element_type=jnp.float32,
    ).reshape(tok_rows, head_count, level_count)
    log_total = jnp.cumsum(log_decay, axis=0)
    doc_stretch = jnp.cumsum(doc_start)
    doc_count = jnp.broadcast_to(doc_stretch[:, None], (per_span, STRETCH)).reshape(tok_rows)
    scaled_in = (jnp.repeat(step_size, head_width, axis=1) * values_in.astype(jnp.float32)).astype(
        jnp.bfloat16
    )
    end_log = log_total[tok_rows - 1]
    tail_decay = (
        jnp.exp(end_log[None, :] - log_total)
        * (doc_count == doc_count[tok_rows - 1]).astype(jnp.float32)[:, None]
    )
    carried_in = (
        jnp.repeat(tail_decay, head_width, axis=1) * scaled_in.astype(jnp.float32)
    ).astype(jnp.bfloat16)
    end_state = jnp.einsum("sc,sn->cn", carried_in, key_proj, preferred_element_type=jnp.float32)
    span_decay = jnp.exp(end_log) * (doc_count[tok_rows - 1] == 0).astype(jnp.float32)
    own_index = lax.axis_index(SEQ)
    row_share = head_count * head_width // span_total
    pieces = lax.all_to_all(
        end_state.reshape(1, head_count * head_width, state_width).astype(jnp.bfloat16),
        SEQ,
        split_axis=1,
        concat_axis=0,
        tiled=True,
    ).astype(jnp.float32)
    decays = gathered_by_axis(span_decay.reshape(1, head_count), SEQ, (0, 1, 2), 0)
    row_head = (own_index * row_share + jnp.arange(row_share, dtype=jnp.int32)) // head_width
    head_pick = (row_head[:, None] == jnp.arange(head_count, dtype=jnp.int32)[None, :]).astype(
        jnp.float32
    )
    block_decay = jnp.dot(
        decays, head_pick.T, precision=lax.Precision.HIGHEST, preferred_element_type=jnp.float32
    )
    block_state = pieces
    lead_decay = jnp.ones_like(block_decay)
    span_range = jnp.arange(span_total, dtype=jnp.int32)
    level_list = []
    for bit_index in range(span_bits):
        other_state = flip_pairs(block_state, bit_index)
        other_decay = flip_pairs(block_decay, bit_index)
        is_upper = span_range >> bit_index & 1 == 1
        level_list.append(
            jnp.where(is_upper[:, None, None], lead_decay[:, :, None] * other_state, 0.0)
        )
        block_state = jnp.where(
            is_upper[:, None, None],
            block_state + block_decay[:, :, None] * other_state,
            other_state + other_decay[:, :, None] * block_state,
        )
        lead_decay = jnp.where(is_upper[:, None], lead_decay * other_decay, lead_decay)
        block_decay = block_decay * other_decay
    level_all = jnp.stack(level_list, 1).astype(jnp.bfloat16)
    returned = lax.all_to_all(level_all, SEQ, split_axis=0, concat_axis=2, tiled=True)
    remote_state = returned.reshape(span_bits, head_count, head_width, state_width)
    level_index = level_of_pairs(tok_rows, STRETCH, low_bits)
    element_position = jnp.arange(tok_rows, dtype=jnp.int32)
    visible = (element_position[:, None] >= element_position[None, :]) & (
        doc_count[:, None] == doc_count[None, :]
    )
    scores = jnp.einsum("tn,sn->ts", query_proj, key_proj, preferred_element_type=jnp.float32)
    reach_decay = jnp.exp(log_total) * (doc_count == 0).astype(jnp.float32)[:, None]
    group_size = math.gcd(head_count, 4)
    group_count = head_count // group_size

    def head_group(inputs):
        group_log, group_weight, group_scaled, group_remote, group_reach = inputs
        select = jnp.zeros((group_size, tok_rows, tok_rows), jnp.float32)
        for level_id in range(low_bits + 1):
            select = select + jnp.where(
                level_index[None] == level_id,
                jnp.transpose(group_weight[:, :, level_id])[:, :, None],
                0.0,
            )
        log_rows = jnp.transpose(group_log)
        log_gap = jnp.where(visible[None], log_rows[:, :, None] - log_rows[:, None, :], -jnp.inf)
        mixing = (scores[None] * select * jnp.exp(log_gap)).astype(jnp.bfloat16)
        local_part = jnp.einsum(
            "hts,shp->thp",
            mixing,
            group_scaled.reshape(tok_rows, group_size, head_width),
            preferred_element_type=jnp.float32,
        )
        projected = jnp.einsum(
            "tn,bhpn->tbhp", query_proj, group_remote, preferred_element_type=jnp.float32
        )
        remote_weight = group_weight[:, :, 1 + low_bits : 1 + low_bits + span_bits]
        remote_part = group_reach[:, :, None] * jnp.einsum(
            "thb,tbhp->thp", remote_weight, projected, precision=lax.Precision.HIGHEST
        )
        return (local_part + remote_part).reshape(tok_rows, group_size * head_width)

    stacked = (
        log_total.reshape(tok_rows, group_count, group_size).transpose(1, 0, 2),
        level_weight.reshape(tok_rows, group_count, group_size, level_count).transpose(1, 0, 2, 3),
        scaled_in.reshape(tok_rows, group_count, group_size * head_width).transpose(1, 0, 2),
        remote_state.reshape(span_bits, group_count, group_size, head_width, state_width).transpose(
            1, 0, 2, 3, 4
        ),
        reach_decay.reshape(tok_rows, group_count, group_size).transpose(1, 0, 2),
    )
    group_parts = lax.map(head_group, stacked)
    both_parts = group_parts.transpose(1, 0, 2).reshape(tok_rows, head_count * head_width)
    combined = both_parts + jnp.repeat(skip_weight, head_width)[None, :] * values_in.astype(
        jnp.float32
    )
    gated_out = combined * jax.nn.silu(gate_in.astype(jnp.float32))
    square_sum = over_copies(jnp.sum(gated_out * gated_out, axis=1), "head")
    mean_square = square_sum / (H * HEADDIM)
    return (gated_out * lax.rsqrt(mean_square + epsilon)[:, None] * norm_gain[None, :]).astype(
        jnp.bfloat16
    )


def solution(mesh):
    split = Mesh(
        mesh.devices.reshape(4, 16, 2, mesh.shape["head"]), ("seq_0", "seq_1", "seq_2", "head")
    )
    placed = (
        P(SEQ, "head"),
        P(SEQ, "head"),
        P(SEQ, None),
        P(SEQ, None),
        P(SEQ, "head"),
        P(SEQ, "head"),
        P("head"),
        P("head"),
        P(None, "head", None),
        P(SEQ),
        P(SEQ),
    )
    return jax.shard_map(
        local, mesh=split, in_specs=placed, out_specs=P(SEQ, "head"), check_vma=False
    )
```

profile of v0, /device:TPU:2, one launch (start us, length us, event | category | flops | bytes accessed | tf_op | source)
XLA Modules:
  0.0 271.4 jit_solution(7450920758946439737)
XLA Ops:
  3.7 1.1 reduce-window.19
  5.1 1.5 copy.349
  7.6 1.4 fusion.30
  10.4 2.2 reduce.9
  13.4 19.5 %all-to-all-start = ((bf16[128,2,512]{2,1,0:T(2,128)(2,1)}), bf16[128,2,512]{2,1,0:T(2,128)(2,1)S(1)}, u32[]{:S(2)}, u32[]{:S(2)}) async-start(bf16[128,2,512]{2,1,0:T(2,128)(2,1)} %reshape.1288), calls=%async_computation | async-start | bytes 524288 | tf_op jit(solution)/shard_map/all_to_all | solution.py:113
  33.1 8.0 %all-gather.3 = f32[4,1,16]{2,1,0:T(1,128)S(1)} all-gather(f32[1,1,16]{2,1,0:T(1,128)S(1)} %bitcast.339), channel_id=2, replica_groups=mesh['seq_0'=4,'seq_1'=16,'seq_2'=2,'head'=4] {'seq_0'}, dimensions={0}, use_global_device_ids=true | all-gather | bytes 320 | tf_op jit(solution)/shard_map/all_gather | solution.py:24
  41.1 29.5 %all-gather.4 = f32[16,4,16]{2,1,0:T(4,128)S(1)} all-gather(f32[1,4,16]{2,1,0:T(4,128)S(1)} %bitcast.338), channel_id=3, replica_groups=mesh['seq_0'=4,'seq_1'=16,'seq_2'=2,'head'=4] {'seq_1'}, dimensions={0}, use_global_device_ids=true | all-gather | bytes 4352 | tf_op jit(solution)/shard_map/all_gather | solution.py:24
  70.7 2.0 all-gather.5
  87.5 1.0 add_select_fusion.4
  88.6 2.5 add_select_fusion.3
  91.0 1.1 rev.45
  92.1 2.8 %add_select_fusion.2 = f32[4,2,16,8,128]{4,3,2,1,0:T(8,128)} fusion(f32[4,2,16,8,128]{4,3,2,1,0:T(8,128)S(1)} %bitcast.269, f32[4,2,16,8,128]{4,3,2,1,0:T(8,128)S(1)} %bitcast.265, f32[4,2,16,8,128]{4,3,2,1,0:T(8,128)S(1)} %bitcast.260, f32[4,2,16,8,128]{4,3,2,1,0:T(8,128)S(1)} %bitcast.247, f32[4,2,16,8,128]{4,3,2,1,0:T(8,128)S(1)} %bitcast.255, ...), kind=kLoop, calls=%fused_computation.60 | loop fusion | flops 2621440 | bytes 3179008 | tf_op jit(solution)/shard_map/jit(_where)/select_n | solution.py:139
  94.9 1.1 rev.47
  96.0 5.8 %add_select_fusion.1 = f32[2,2,32,8,128]{4,3,2,1,0:T(8,128)} fusion(f32[2,2,32,8,128]{4,3,2,1,0:T(8,128)S(1)} %bitcast.274, f32[2,2,32,8,128]{4,3,2,1,0:T(8,128)S(1)} %bitcast.270, f32[2,2,32,8,128]{4,3,2,1,0:T(8,128)S(1)} %bitcast.266, f32[2,2,32,8,128]{4,3,2,1,0:T(8,128)S(1)} %bitcast.261, f32[2,2,32,8,128]{4,3,2,1,0:T(8,128)S(1)} %bitcast.248, ...), kind=kLoop, calls=%fused_computation.58 | loop fusion | flops 3276800 | bytes 3711616 | tf_op jit(solution)/shard_map/jit(_where)/select_n | solution.py:139
  101.8 1.9 rev.49
  103.7 6.6 %add_select_fusion = f32[1,2,64,8,128]{4,3,2,1,0:T(8,128)} fusion(f32[1,2,64,8,128]{4,3,2,1,0:T(8,128)} %bitcast.279, f32[1,2,64,8,128]{4,3,2,1,0:T(8,128)S(1)} %bitcast.275, f32[1,2,64,8,128]{4,3,2,1,0:T(8,128)S(1)} %bitcast.271, f32[1,2,64,8,128]{4,3,2,1,0:T(8,128)S(1)} %bitcast.267, f32[1,2,64,8,128]{4,3,2,1,0:T(8,128)S(1)} %bitcast.262, ...), kind=kLoop, calls=%fused_computation.56 | loop fusion | flops 3932160 | bytes 4244224 | tf_op jit(solution)/shard_map/jit(_where)/select_n | solution.py:139
  110.4 1.9 rev.51
  112.3 0.9 fusion.32
  113.3 2.0 fusion.33
  115.2 1.1 fusion.34
  116.3 1.1 fusion.35
  117.4 1.1 fusion.36
  118.5 1.1 fusion.37
  119.6 1.1 fusion.38
  120.7 14.1 %all-to-all-start.1 = ((bf16[128,7,8,128]{3,2,1,0:T(8,128)(2,1)}), bf16[128,7,8,128]{3,2,1,0:T(8,128)(2,1)S(1)}, u32[]{:S(2)}, u32[]{:S(2)}) async-start(bf16[128,7,8,128]{3,2,1,0:T(8,128)(2,1)} %fusion.38), calls=%async_computation.1 | async-start | bytes 3670016 | tf_op jit(solution)/shard_map/all_to_all | solution.py:147
  136.0 1.3 copy.411
  137.5 1.2 fusion.50
  138.7 84.2 %all-to-all-done.1 = bf16[128,7,8,128]{3,2,1,0:T(8,128)(2,1)S(1)} async-done(((bf16[128,7,8,128]{3,2,1,0:T(8,128)(2,1)}), bf16[128,7,8,128]{3,2,1,0:T(8,128)(2,1)S(1)}, u32[]{:S(2)}, u32[]{:S(2)}) %all-to-all-start.1) | async-done | bytes 1835040 | tf_op jit(solution)/shard_map/all_to_all | solution.py:147
  222.9 1.6 copy.408
  224.5 32.9 %while.12 = (s32[]{:T(128)}, f32[4,512,256]{1,2,0:T(8,128)}, bf16[4,512,256]{1,2,0:T(8,128)(2,1)}, f32[512,512]{1,0:T(8,128)S(1)}, f32[4,512,4,11]{1,2,3,0:T(4,1...) while((s32[]{:T(128)}, f32[4,512,256]{1,2,0:T(8,128)}, ...), condition=%wide.region_4.5_spmd.clone.clone, body=%wide.region_3.4_spmd.clone.clone.sunk | while | flops 387842048 | bytes 8172673 | solution.py:195
  224.5 1.8 fusion.70
  226.4 1.0 constant_dynamic-slice_fusion.2
  227.3 0.9 fusion.69
  228.5 3.4 %fusion.71 = f32[512,4,64]{0,2,1:T(8,128)S(1)} fusion(bf16[512,4,64]{0,2,1:T(8,128)(2,1)S(1)} %bitcast.277, f32[4,512]{1,0:T(4,128)S(1)} %get-tuple-element.349, f32[4,512]{1,0:T(4,128)S(1)} %get-tuple-element.350, f32[4,512]{1,0:T(4,128)S(1)} %get-tuple-element.351, f32[4,512]{1,0:T(4,128)S(1)} %get-tuple-element.352, ...), kind=kOutput, calls=%fused_computation.15.clone.1 | convolution fusion | flops 147062784 | bytes 3719168 | tf_op jit(solution)/shard_map/while/body/eval_jaxpr/hts,shp->thp/dot_general | solution.py:171
  232.8 1.7 fusion.70
  234.6 1.0 constant_dynamic-slice_fusion.2
  235.6 0.9 fusion.69
  236.7 3.4 %fusion.71 = f32[512,4,64]{0,2,1:T(8,128)S(1)} fusion(bf16[512,4,64]{0,2,1:T(8,128)(2,1)S(1)} %bitcast.277, f32[4,512]{1,0:T(4,128)S(1)} %get-tuple-element.349, f32[4,512]{1,0:T(4,128)S(1)} %get-tuple-element.350, f32[4,512]{1,0:T(4,128)S(1)} %get-tuple-element.351, f32[4,512]{1,0:T(4,128)S(1)} %get-tuple-element.352, ...), kind=kOutput, calls=%fused_computation.15.clone.1 | convolution fusion | flops 147062784 | bytes 3719168 | tf_op jit(solution)/shard_map/while/body/eval_jaxpr/hts,shp->thp/dot_general | solution.py:171
  241.0 1.7 fusion.70
  242.8 1.0 constant_dynamic-slice_fusion.2
  244.9 3.4 %fusion.71 = f32[512,4,64]{0,2,1:T(8,128)S(1)} fusion(bf16[512,4,64]{0,2,1:T(8,128)(2,1)S(1)} %bitcast.277, f32[4,512]{1,0:T(4,128)S(1)} %get-tuple-element.349, f32[4,512]{1,0:T(4,128)S(1)} %get-tuple-element.350, f32[4,512]{1,0:T(4,128)S(1)} %get-tuple-element.351, f32[4,512]{1,0:T(4,128)S(1)} %get-tuple-element.352, ...), kind=kOutput, calls=%fused_computation.15.clone.1 | convolution fusion | flops 147062784 | bytes 3719168 | tf_op jit(solution)/shard_map/while/body/eval_jaxpr/hts,shp->thp/dot_general | solution.py:171
  249.2 1.7 fusion.70
  251.0 1.0 constant_dynamic-slice_fusion.2
  252.0 0.9 fusion.69
  253.1 3.4 %fusion.71 = f32[512,4,64]{0,2,1:T(8,128)S(1)} fusion(bf16[512,4,64]{0,2,1:T(8,128)(2,1)S(1)} %bitcast.277, f32[4,512]{1,0:T(4,128)S(1)} %get-tuple-element.349, f32[4,512]{1,0:T(4,128)S(1)} %get-tuple-element.350, f32[4,512]{1,0:T(4,128)S(1)} %get-tuple-element.351, f32[4,512]{1,0:T(4,128)S(1)} %get-tuple-element.352, ...), kind=kOutput, calls=%fused_computation.15.clone.1 | convolution fusion | flops 147062784 | bytes 3719168 | tf_op jit(solution)/shard_map/while/body/eval_jaxpr/hts,shp->thp/dot_general | solution.py:171
  257.4 2.8 %multiply_reduce_fusion = (f32[512]{0:T(512)S(1)}, f32[512,1024]{0,1:T(8,128)S(1)}) fusion(bf16[512,1024]{0,1:T(8,128)(2,1)} %copy.411, bf16[512,1024]{0,1:T(8,128)(2,1)S(1)} %copy-done.2, f32[1024]{0:T(1024)S(1)} %mul.848, f32[4,512,256]{1,2,0:T(8,128)} %get-tuple-element.71), kind=kLoop, calls=%fused_computation.51 | loop fusion | flops 5766656 | bytes 6297600 | tf_op jit(solution)/shard_map/reduce_sum | solution.py:201
  260.2 9.6 %all_to_all.30 = f32[4,1,512]{2,1,0:T(1,128)S(1)} all-to-all(f32[4,1,512]{2,1,0:T(1,128)S(1)} %broadcast_in_dim.337), channel_id=1, replica_groups=mesh['seq_0'=4,'seq_1'=16,'seq_2'=2,'head'=4] {'head'}, dimensions={0} | all-to-all | bytes 16384 | tf_op jit(solution)/shard_map/all_to_all | solution.py:37
  270.1 1.3 copy.413
  (200 shorter events, 28.2 us)
Async XLA Ops:
  0.0 9.0 %copy-start = (bf16[512,128]{1,0:T(8,128)(2,1)S(1)}, bf16[512,128]{1,0:T(8,128)(2,1)}, u32[]{:S(2)}) copy-start(bf16[512,128]{1,0:T(8,128)(2,1)} %param.15) | copy-start | bytes 393220
  0.0 7.6 %copy-start.19 = (f32[512,16]{0,1:T(8,128)S(1)}, f32[512,16]{0,1:T(8,128)}, u32[]{:S(2)}) copy-start(f32[512,16]{0,1:T(8,128)} %param.17) | copy-start | bytes 98308
  5.1 3.9 %copy-start.15 = (f32[512,16]{0,1:T(8,128)}, f32[512,16]{0,1:T(8,128)S(1)}, u32[]{:S(2)}) copy-start(f32[512,16]{0,1:T(8,128)S(1)} %bitcast_bitcast_fusion) | copy-start | bytes 98308
  6.6 2.8 %copy-start.1 = (bf16[512,1024]{0,1:T(8,128)(2,1)}, bf16[512,1024]{0,1:T(8,128)(2,1)S(1)}, u32[]{:S(2)}) copy-start(bf16[512,1024]{0,1:T(8,128)(2,1)S(1)} %copy.349) | copy-start | bytes 3145732
  13.4 72.8 %all-to-all-start = ((bf16[128,2,512]{2,1,0:T(2,128)(2,1)}), bf16[128,2,512]{2,1,0:T(2,128)(2,1)S(1)}, u32[]{:S(2)}, u32[]{:S(2)}) async-start(bf16[128,2,512]{2,1,0:T(2,128)(2,1)} %reshape.1288), calls=%async_computation | async-start | bytes 524288 | tf_op jit(solution)/shard_map/all_to_all | solution.py:113
  33.0 41.8 %copy-start.22 = (pred[128]{0:T(512)(128)(4,1)}, pred[128]{0:T(512)(128)(4,1)S(1)}, u32[]{:S(2)}) copy-start(pred[128]{0:T(512)(128)(4,1)S(1)} %get-tuple-element.252) | copy-start | bytes 388
  33.0 41.8 %copy-start.24 = (pred[128]{0:T(512)(128)(4,1)}, pred[128]{0:T(512)(128)(4,1)S(1)}, u32[]{:S(2)}) copy-start(pred[128]{0:T(512)(128)(4,1)S(1)} %get-tuple-element.253) | copy-start | bytes 388
  33.0 41.8 %copy-start.26 = (pred[128]{0:T(512)(128)(4,1)}, pred[128]{0:T(512)(128)(4,1)S(1)}, u32[]{:S(2)}) copy-start(pred[128]{0:T(512)(128)(4,1)S(1)} %get-tuple-element.254) | copy-start | bytes 388
  33.0 41.8 %copy-start.28 = (pred[128]{0:T(512)(128)(4,1)}, pred[128]{0:T(512)(128)(4,1)S(1)}, u32[]{:S(2)}) copy-start(pred[128]{0:T(512)(128)(4,1)S(1)} %get-tuple-element.255) | copy-start | bytes 388
  33.1 41.8 %copy-start.30 = (pred[128]{0:T(512)(128)(4,1)}, pred[128]{0:T(512)(128)(4,1)S(1)}, u32[]{:S(2)}) copy-start(pred[128]{0:T(512)(128)(4,1)S(1)} %get-tuple-element.256) | copy-start | bytes 388
  33.1 41.8 %copy-start.32 = (pred[128]{0:T(512)(128)(4,1)}, pred[128]{0:T(512)(128)(4,1)S(1)}, u32[]{:S(2)}) copy-start(pred[128]{0:T(512)(128)(4,1)S(1)} %get-tuple-element.257) | copy-start | bytes 388
  73.7 18.4 %copy-start.4 = (f32[128,8]{1,0:T(8,128)}, f32[128,8]{1,0:T(8,128)S(1)}, u32[]{:S(2)}) copy-start(f32[128,8]{1,0:T(8,128)S(1)} %copy.374) | copy-start | bytes 12292
  73.7 18.4 %copy-start.5 = (f32[16,2,4,8]{3,2,1,0:T(4,128)}, f32[16,2,4,8]{3,2,1,0:T(4,128)S(1)}, u32[]{:S(2)}) copy-start(f32[16,2,4,8]{3,2,1,0:T(4,128)S(1)} %rev.44) | copy-start | bytes 12292
  75.0 17.1 %copy-start.7 = (f32[8,2,8,8]{3,2,1,0:T(8,128)}, f32[8,2,8,8]{3,2,1,0:T(8,128)S(1)}, u32[]{:S(2)}) copy-start(f32[8,2,8,8]{3,2,1,0:T(8,128)S(1)} %copy.429) | copy-start | bytes 12292
  75.1 17.1 %copy-start.8 = (f32[128,8]{1,0:T(8,128)}, f32[128,8]{1,0:T(8,128)S(1)}, u32[]{:S(2)}) copy-start(f32[128,8]{1,0:T(8,128)S(1)} %copy.428) | copy-start | bytes 12292
  103.7 8.6 %copy-start.33 = (pred[128]{0:T(512)(128)(4,1)S(1)}, pred[128]{0:T(512)(128)(4,1)}, u32[]{:S(2)}) copy-start(pred[128]{0:T(512)(128)(4,1)} %copy-done.32) | copy-start | bytes 388
  103.7 9.5 %copy-start.31 = (pred[128]{0:T(512)(128)(4,1)S(1)}, pred[128]{0:T(512)(128)(4,1)}, u32[]{:S(2)}) copy-start(pred[128]{0:T(512)(128)(4,1)} %copy-done.30) | copy-start | bytes 388
  110.3 4.9 %copy-start.14 = (f32[128,8]{1,0:T(8,128)S(1)}, f32[128,8]{1,0:T(8,128)}, u32[]{:S(2)}) copy-start(f32[128,8]{1,0:T(8,128)} %copy.366) | copy-start | bytes 12292
  110.3 4.9 %copy-start.29 = (pred[128]{0:T(512)(128)(4,1)S(1)}, pred[128]{0:T(512)(128)(4,1)}, u32[]{:S(2)}) copy-start(pred[128]{0:T(512)(128)(4,1)} %copy-done.28) | copy-start | bytes 388
  110.3 6.0 %copy-start.13 = (f32[128,8]{1,0:T(8,128)S(1)}, f32[128,8]{1,0:T(8,128)}, u32[]{:S(2)}) copy-start(f32[128,8]{1,0:T(8,128)} %copy.376) | copy-start | bytes 12292
  110.3 6.0 %copy-start.27 = (pred[128]{0:T(512)(128)(4,1)S(1)}, pred[128]{0:T(512)(128)(4,1)}, u32[]{:S(2)}) copy-start(pred[128]{0:T(512)(128)(4,1)} %copy-done.26) | copy-start | bytes 388
  110.3 7.1 %copy-start.12 = (f32[128,8]{1,0:T(8,128)S(1)}, f32[128,8]{1,0:T(8,128)}, u32[]{:S(2)}) copy-start(f32[128,8]{1,0:T(8,128)} %copy.384) | copy-start | bytes 12292
  110.4 7.1 %copy-start.25 = (pred[128]{0:T(512)(128)(4,1)S(1)}, pred[128]{0:T(512)(128)(4,1)}, u32[]{:S(2)}) copy-start(pred[128]{0:T(512)(128)(4,1)} %copy-done.24) | copy-start | bytes 388
  112.3 6.2 %copy-start.3 = (f32[2,2,32,8,128]{4,3,2,1,0:T(8,128)S(1)}, f32[2,2,32,8,128]{4,3,2,1,0:T(8,128)}, u32[]{:S(2)}) copy-start(f32[2,2,32,8,128]{4,3,2,1,0:T(8,128)} %rev.49) | copy-start | bytes 1572868
  112.3 6.2 %copy-start.11 = (f32[128,8]{1,0:T(8,128)S(1)}, f32[128,8]{1,0:T(8,128)}, u32[]{:S(2)}) copy-start(f32[128,8]{1,0:T(8,128)} %copy.390) | copy-start | bytes 12292
  112.3 6.2 %copy-start.23 = (pred[128]{0:T(512)(128)(4,1)S(1)}, pred[128]{0:T(512)(128)(4,1)}, u32[]{:S(2)}) copy-start(pred[128]{0:T(512)(128)(4,1)} %copy-done.22) | copy-start | bytes 388
  113.3 6.3 %copy-start.6 = (f32[1,2,64,8,128]{4,3,2,1,0:T(8,128)S(1)}, f32[1,2,64,8,128]{4,3,2,1,0:T(8,128)}, u32[]{:S(2)}) copy-start(f32[1,2,64,8,128]{4,3,2,1,0:T(8,128)} %rev.51) | copy-start | bytes 1572868
  113.3 6.3 %copy-start.10 = (f32[128,8]{1,0:T(8,128)S(1)}, f32[128,8]{1,0:T(8,128)}, u32[]{:S(2)}) copy-start(f32[128,8]{1,0:T(8,128)} %copy.398) | copy-start | bytes 12292
  113.3 6.3 %copy-start.34 = (pred[128]{0:T(512)(128)(4,1)S(1)}, pred[128]{0:T(512)(128)(4,1)}, u32[]{:S(2)}) copy-start(pred[128]{0:T(512)(128)(4,1)} %and_compare_fusion.21) | copy-start | bytes 388
  119.6 15.2 %copy-start.16 = (f32[512,16]{0,1:T(8,128)S(1)}, f32[512,16]{0,1:T(8,128)}, u32[]{:S(2)}) copy-start(f32[512,16]{0,1:T(8,128)} %copy-done.15) | copy-start | bytes 98308
  119.6 15.2 %copy-start.17 = (f32[512,16]{0,1:T(8,128)S(1)}, f32[512,16]{0,1:T(8,128)}, u32[]{:S(2)}) copy-start(f32[512,16]{0,1:T(8,128)} %get-tuple-element.248) | copy-start | bytes 98308
  120.6 14.2 %copy-start.18 = (f32[16,16,11]{1,0,2:T(8,128)S(1)}, f32[16,16,11]{1,0,2:T(8,128)}, u32[]{:S(2)}) copy-start(f32[16,16,11]{1,0,2:T(8,128)} %param.21) | copy-start | bytes 33796
  120.7 14.7 %copy-start.21 = (s32[512]{0:T(512)S(1)}, s32[512]{0:T(512)}, u32[]{:S(2)}) copy-start(s32[512]{0:T(512)} %param.22) | copy-start | bytes 6148
  120.7 15.3 %copy-start.9 = (bf16[512,1024]{1,0:T(8,128)(2,1)S(1)}, bf16[512,1024]{1,0:T(8,128)(2,1)}, u32[]{:S(2)}) copy-start(bf16[512,1024]{1,0:T(8,128)(2,1)} %param.14) | copy-start | bytes 3145732
  120.7 102.3 %all-to-all-start.1 = ((bf16[128,7,8,128]{3,2,1,0:T(8,128)(2,1)}), bf16[128,7,8,128]{3,2,1,0:T(8,128)(2,1)S(1)}, u32[]{:S(2)}, u32[]{:S(2)}) async-start(bf16[128,7,8,128]{3,2,1,0:T(8,128)(2,1)} %fusion.38), calls=%async_computation.1 | async-start | bytes 3670016 | tf_op jit(solution)/shard_map/all_to_all | solution.py:147
  134.8 2.5 copy-start.35
  224.5 32.9 %copy-start.2 = (bf16[512,1024]{0,1:T(8,128)(2,1)S(1)}, bf16[512,1024]{0,1:T(8,128)(2,1)}, u32[]{:S(2)}) copy-start(bf16[512,1024]{0,1:T(8,128)(2,1)} %copy-done.1) | copy-start | bytes 3145732
  257.4 12.4 %copy-start.20 = (f32[1024]{0:T(1024)S(1)}, f32[1024]{0:T(1024)}, u32[]{:S(2)}) copy-start(f32[1024]{0:T(1024)} %param.20) | copy-start | bytes 12292
where the time goes:
time: 273 us; the launch traced here: 271 us
  waiting for transfers between devices  84.2 us (31%)
  blocking collectives  49.1 us (18%)
  other arithmetic  46.5 us (17%)
  starting transfers between devices  33.6 us (12%)
  local copies, waits for them, and re-layouts  33.5 us (12%)
  matrix products  22.9 us (8%)
    all_to_all x1, waiting for transfers between devices, local(): lax.all_to_all(level_all, SEQ, split_axis=0, concat_axis=2, tiled=True)  84.2 us
    all_gather x3, blocking collectives, gather_in_order(): pieces = lax.all_gather(pieces, axes[k], axis=0, tiled=True)  39.5 us
    all_to_all x1, starting transfers between devices, local(): lax.all_to_all(end_state.reshape(1, head_count * head_width, state_width)...  19.5 us
    select_n x6, other arithmetic, local(): jnp.where(is_upper[:, None, None], block_state + block_decay[:, :, None]...  19.1 us
    all_to_all x1, starting transfers between devices, local(): lax.all_to_all(level_all, SEQ, split_axis=0, concat_axis=2, tiled=True)  14.1 us
    dot_general x4, matrix products, head_group(): jnp.einsum('hts,shp->thp', mixing, group_scaled.reshape(tok_rows, group_s...  13.7 us
    all_to_all x1, blocking collectives, copy_for_each(): lax.all_to_all(jnp.broadcast_to(array[None], (size, *array.shape)), axis,...  9.6 us
    unnamed x7, other arithmetic  9.43 us
  transfers between devices with their start and end apart: 2, of which 1 were waited for; matrix products, arithmetic and copies ran while one was open for 6% of the time, Pallas kernels for 0%

commit v1 on v0

--- a/solution.py
+++ b/solution.py
@@ -12,6 +12,13 @@
 epsilon = 1e-06
 
 
+def gather_over(x, axis, dim):
+    size = lax.axis_size(axis)
+    tiles = jnp.stack([x for _ in range(size)])
+    tiles = lax.all_to_all(tiles, axis, split_axis=0, concat_axis=0)
+    return jnp.concatenate(tiles, axis=dim)
+
+
 def joined_along(pieces, dim):
     pieces = jnp.moveaxis(pieces, 0, dim)
     shape = pieces.shape
@@ -21,7 +28,7 @@
 def gather_in_order(array, axes, turns):
     pieces = array[None]
     for k in turns:
-        pieces = lax.all_gather(pieces, axes[k], axis=0, tiled=True)
+        pieces = gather_over(pieces, axes[k], 0)
     current = [lax.axis_size(axes[k]) for k in reversed(turns)]
     pieces = pieces.reshape(*current, *array.shape)
     turned = sorted(range(len(turns)), key=lambda place: turns[len(turns) - 1 - place])

time: 273 us -> 261 us (0.956)
  blocking collectives: 49.1 us -> 13.3 us
  waiting for transfers between devices: 84.2 us -> 103 us
    all_gather x3 -> x0, blocking collectives: 39.5 us -> none  [gather_in_order(): pieces = lax.all_gather(pieces, axes[k], axis=0, tiled=True)]
    all_to_all x0 -> x2, starting transfers between devices: none -> 20 us  [gather_over(): tiles = lax.all_to_all(tiles, axis, split_axis=0, concat_axis=0)]
    all_to_all x1, starting transfers between devices: 19.5 us -> 8.14 us  [local(): lax.all_to_all(end_state.reshape(1, head_count * head_width, state_width)...]
    all_to_all x1, waiting for transfers between devices: 0.01 us -> 10.9 us  [local(): lax.all_to_all(end_state.reshape(1, head_count * head_width, state_width)...]
    all_to_all x0 -> x2, waiting for transfers between devices: none -> 8.2 us  [gather_over(): tiles = lax.all_to_all(tiles, axis, split_axis=0, concat_axis=0)]
    all_to_all x1, starting transfers between devices: 14.1 us -> 7.33 us  [local(): lax.all_to_all(level_all, SEQ, split_axis=0, concat_axis=2, tiled=True)]
    all_to_all x0 -> x1, blocking collectives: none -> 3.71 us  [gather_over(): tiles = lax.all_to_all(tiles, axis, split_axis=0, concat_axis=0)]
    unnamed x7 -> x8, other arithmetic: 9.43 us -> 9.43 us
  transfers between devices with their start and end apart: 2 -> 4, of which waited for: 1 -> 3; matrix products, arithmetic and copies ran while one was open for 6% -> 10% of each run, Pallas kernels for 0% -> 0%
where the time goes in v1:
time: 261 us; the launch traced here: 259 us
  waiting for transfers between devices  103 us (39%)
  other arithmetic  47 us (18%)
  local copies, waits for them, and re-layouts  35.5 us (14%)
  starting transfers between devices  35.5 us (14%)
  matrix products  22.9 us (9%)
  blocking collectives  13.3 us (5%)
    all_to_all x1, waiting for transfers between devices, local(): lax.all_to_all(level_all, SEQ, split_axis=0, concat_axis=2, tiled=True)  84.2 us
    all_to_all x2, starting transfers between devices, gather_over(): tiles = lax.all_to_all(tiles, axis, split_axis=0, concat_axis=0)  20 us
    select_n x6, other arithmetic, local(): jnp.where(is_upper[:, None, None], block_state + block_decay[:, :, None]...  19.1 us
    dot_general x4, matrix products, head_group(): jnp.einsum('hts,shp->thp', mixing, group_scaled.reshape(tok_rows, group_s...  13.7 us
    all_to_all x1, waiting for transfers between devices, local(): lax.all_to_all(end_state.reshape(1, head_count * head_width, state_width)...  10.9 us
    all_to_all x1, blocking collectives, copy_for_each(): lax.all_to_all(jnp.broadcast_to(array[None], (size, *array.shape)), axis,...  9.58 us
    unnamed x8, other arithmetic  9.43 us
    all_to_all x2, waiting for transfers between devices, gather_over(): tiles = lax.all_to_all(tiles, axis, split_axis=0, concat_axis=0)  8.2 us
  transfers between devices with their start and end apart: 4, of which 3 were waited for; matrix products, arithmetic and copies ran while one was open for 10% of the time, Pallas kernels for 0%

profile of v1, /device:TPU:2, one launch (start us, length us, event | category | flops | bytes accessed | tf_op | source)
XLA Modules:
  0.0 259.0 jit_solution(9100354014568095125)
XLA Ops:
  2.4 1.1 reduce-window.19
  5.3 9.1 %all-to-all-start.1 = ((f32[4,1,1,16]{3,2,1,0:T(1,128)}), f32[4,1,1,16]{3,2,1,0:T(1,128)S(1)}, u32[]{:S(2)}, u32[]{:S(2)}) async-start(f32[4,1,1,16]{3,2,1,0:T(1,128)} %stack.9), calls=%async_computation.1 | async-start | bytes 4096 | tf_op jit(solution)/shard_map/all_to_all | solution.py:18
  17.4 1.5 copy.352
  19.7 1.4 fusion.30
  22.2 10.9 %all-to-all-start.2 = ((f32[16,4,1,16]{3,1,2,0:T(4,128)}), f32[16,4,1,16]{3,1,2,0:T(4,128)S(1)}, u32[]{:S(2)}, u32[]{:S(2)}) async-start(f32[16,4,1,16]{3,1,2,0:T(4,128)} %stack.10), calls=%async_computation.2 | async-start | bytes 65536 | tf_op jit(solution)/shard_map/all_to_all | solution.py:18
  34.6 2.2 reduce.7
  37.6 8.2 %all-to-all-done.2 = f32[16,4,1,16]{3,1,2,0:T(4,128)S(1)} async-done(((f32[16,4,1,16]{3,1,2,0:T(4,128)}), f32[16,4,1,16]{3,1,2,0:T(4,128)S(1)}, u32[]{:S(2)}, u32[]{:S(2)}) %all-to-all-start.2) | async-done | bytes 4128 | tf_op jit(solution)/shard_map/all_to_all | solution.py:18
  45.9 3.7 %all_to_all.45 = f32[2,1,1024]{2,1,0:T(1,128)S(1)} all-to-all(f32[2,1,1024]{2,1,0:T(1,128)S(1)} %reshape.1269), channel_id=1, replica_groups=mesh['seq_0'=4,'seq_1'=16,'seq_2'=2,'head'=4] {'seq_2'}, dimensions={0} | all-to-all | bytes 16384 | tf_op jit(solution)/shard_map/all_to_all | solution.py:18
  49.6 8.1 %all-to-all-start = ((bf16[128,2,512]{2,1,0:T(2,128)(2,1)}), bf16[128,2,512]{2,1,0:T(2,128)(2,1)S(1)}, u32[]{:S(2)}, u32[]{:S(2)}) async-start(bf16[128,2,512]{2,1,0:T(2,128)(2,1)} %reshape.1267), calls=%async_computation | async-start | bytes 524288 | tf_op jit(solution)/shard_map/all_to_all | solution.py:120
  69.7 10.9 %all-to-all-done = bf16[128,2,512]{2,1,0:T(2,128)(2,1)S(1)} async-done(((bf16[128,2,512]{2,1,0:T(2,128)(2,1)}), bf16[128,2,512]{2,1,0:T(2,128)(2,1)S(1)}, u32[]{:S(2)}, u32[]{:S(2)}) %all-to-all-start) | async-done | bytes 262176 | tf_op jit(solution)/shard_map/all_to_all | solution.py:120
  81.9 1.0 add_select_fusion.4
  82.9 2.5 add_select_fusion.3
  85.4 1.1 rev.45
  86.5 2.8 %add_select_fusion.2 = f32[4,2,16,8,128]{4,3,2,1,0:T(8,128)} fusion(f32[4,2,16,8,128]{4,3,2,1,0:T(8,128)S(1)} %bitcast.271, f32[4,2,16,8,128]{4,3,2,1,0:T(8,128)S(1)} %bitcast.267, f32[4,2,16,8,128]{4,3,2,1,0:T(8,128)S(1)} %bitcast.262, f32[4,2,16,8,128]{4,3,2,1,0:T(8,128)S(1)} %bitcast.249, f32[4,2,16,8,128]{4,3,2,1,0:T(8,128)S(1)} %bitcast.257, ...), kind=kLoop, calls=%fused_computation.60 | loop fusion | flops 2621440 | bytes 3179008 | tf_op jit(solution)/shard_map/jit(_where)/select_n | solution.py:146
  89.3 1.1 rev.47
  90.3 5.8 %add_select_fusion.1 = f32[2,2,32,8,128]{4,3,2,1,0:T(8,128)} fusion(f32[2,2,32,8,128]{4,3,2,1,0:T(8,128)S(1)} %bitcast.276, f32[2,2,32,8,128]{4,3,2,1,0:T(8,128)S(1)} %bitcast.272, f32[2,2,32,8,128]{4,3,2,1,0:T(8,128)S(1)} %bitcast.268, f32[2,2,32,8,128]{4,3,2,1,0:T(8,128)S(1)} %bitcast.263, f32[2,2,32,8,128]{4,3,2,1,0:T(8,128)S(1)} %bitcast.250, ...), kind=kLoop, calls=%fused_computation.58 | loop fusion | flops 3276800 | bytes 3711616 | tf_op jit(solution)/shard_map/jit(_where)/select_n | solution.py:146
  96.2 1.9 rev.49
  98.1 6.6 %add_select_fusion = f32[1,2,64,8,128]{4,3,2,1,0:T(8,128)} fusion(f32[1,2,64,8,128]{4,3,2,1,0:T(8,128)} %bitcast.281, f32[1,2,64,8,128]{4,3,2,1,0:T(8,128)S(1)} %bitcast.277, f32[1,2,64,8,128]{4,3,2,1,0:T(8,128)S(1)} %bitcast.273, f32[1,2,64,8,128]{4,3,2,1,0:T(8,128)S(1)} %bitcast.269, f32[1,2,64,8,128]{4,3,2,1,0:T(8,128)S(1)} %bitcast.264, ...), kind=kLoop, calls=%fused_computation.56 | loop fusion | flops 3932160 | bytes 4244224 | tf_op jit(solution)/shard_map/jit(_where)/select_n | solution.py:146
  104.7 1.9 rev.51
  106.6 1.0 fusion.32
  107.6 2.0 fusion.33
  109.6 1.1 fusion.34
  110.7 1.1 fusion.35
  111.7 1.1 fusion.36
  112.8 1.1 fusion.37
  113.9 1.1 fusion.38
  115.0 7.3 %all-to-all-start.4 = ((bf16[128,7,8,128]{3,2,1,0:T(8,128)(2,1)}), bf16[128,7,8,128]{3,2,1,0:T(8,128)(2,1)S(1)}, u32[]{:S(2)}, u32[]{:S(2)}) async-start(bf16[128,7,8,128]{3,2,1,0:T(8,128)(2,1)} %fusion.38), calls=%async_computation.4 | async-start | bytes 3670016 | tf_op jit(solution)/shard_map/all_to_all | solution.py:154
  123.6 1.3 copy.415
  125.1 1.2 fusion.51
  126.3 84.2 %all-to-all-done.4 = bf16[128,7,8,128]{3,2,1,0:T(8,128)(2,1)S(1)} async-done(((bf16[128,7,8,128]{3,2,1,0:T(8,128)(2,1)}), bf16[128,7,8,128]{3,2,1,0:T(8,128)(2,1)S(1)}, u32[]{:S(2)}, u32[]{:S(2)}) %all-to-all-start.4) | async-done | bytes 1835040 | tf_op jit(solution)/shard_map/all_to_all | solution.py:154
  210.5 1.6 copy.412
  212.1 32.9 %while.12 = (s32[]{:T(128)}, f32[4,512,256]{1,2,0:T(8,128)}, bf16[4,512,256]{1,2,0:T(8,128)(2,1)}, f32[512,512]{1,0:T(8,128)S(1)}, f32[4,512,4,11]{1,2,3,0:T(4,1...) while((s32[]{:T(128)}, f32[4,512,256]{1,2,0:T(8,128)}, ...), condition=%wide.region_4.5_spmd.clone.clone, body=%wide.region_3.4_spmd.clone.clone.sunk | while | flops 387842048 | bytes 8172673 | solution.py:202
  212.1 1.8 fusion.71
  214.0 1.0 constant_dynamic-slice_fusion.2
  214.9 0.9 fusion.70
  216.1 3.4 %fusion.72 = f32[512,4,64]{0,2,1:T(8,128)S(1)} fusion(bf16[512,4,64]{0,2,1:T(8,128)(2,1)S(1)} %bitcast.279, f32[4,512]{1,0:T(4,128)S(1)} %get-tuple-element.347, f32[4,512]{1,0:T(4,128)S(1)} %get-tuple-element.348, f32[4,512]{1,0:T(4,128)S(1)} %get-tuple-element.349, f32[4,512]{1,0:T(4,128)S(1)} %get-tuple-element.350, ...), kind=kOutput, calls=%fused_computation.15.clone.1 | convolution fusion | flops 147062784 | bytes 3719168 | tf_op jit(solution)/shard_map/while/body/eval_jaxpr/hts,shp->thp/dot_general | solution.py:178
  220.4 1.7 fusion.71
  222.1 1.0 constant_dynamic-slice_fusion.2
  224.3 3.4 %fusion.72 = f32[512,4,64]{0,2,1:T(8,128)S(1)} fusion(bf16[512,4,64]{0,2,1:T(8,128)(2,1)S(1)} %bitcast.279, f32[4,512]{1,0:T(4,128)S(1)} %get-tuple-element.347, f32[4,512]{1,0:T(4,128)S(1)} %get-tuple-element.348, f32[4,512]{1,0:T(4,128)S(1)} %get-tuple-element.349, f32[4,512]{1,0:T(4,128)S(1)} %get-tuple-element.350, ...), kind=kOutput, calls=%fused_computation.15.clone.1 | convolution fusion | flops 147062784 | bytes 3719168 | tf_op jit(solution)/shard_map/while/body/eval_jaxpr/hts,shp->thp/dot_general | solution.py:178
  228.6 1.7 fusion.71
  230.3 1.0 constant_dynamic-slice_fusion.2
  232.5 3.4 %fusion.72 = f32[512,4,64]{0,2,1:T(8,128)S(1)} fusion(bf16[512,4,64]{0,2,1:T(8,128)(2,1)S(1)} %bitcast.279, f32[4,512]{1,0:T(4,128)S(1)} %get-tuple-element.347, f32[4,512]{1,0:T(4,128)S(1)} %get-tuple-element.348, f32[4,512]{1,0:T(4,128)S(1)} %get-tuple-element.349, f32[4,512]{1,0:T(4,128)S(1)} %get-tuple-element.350, ...), kind=kOutput, calls=%fused_computation.15.clone.1 | convolution fusion | flops 147062784 | bytes 3719168 | tf_op jit(solution)/shard_map/while/body/eval_jaxpr/hts,shp->thp/dot_general | solution.py:178
  236.8 1.7 fusion.71
  238.6 1.0 constant_dynamic-slice_fusion.2
  240.7 3.4 %fusion.72 = f32[512,4,64]{0,2,1:T(8,128)S(1)} fusion(bf16[512,4,64]{0,2,1:T(8,128)(2,1)S(1)} %bitcast.279, f32[4,512]{1,0:T(4,128)S(1)} %get-tuple-element.347, f32[4,512]{1,0:T(4,128)S(1)} %get-tuple-element.348, f32[4,512]{1,0:T(4,128)S(1)} %get-tuple-element.349, f32[4,512]{1,0:T(4,128)S(1)} %get-tuple-element.350, ...), kind=kOutput, calls=%fused_computation.15.clone.1 | convolution fusion | flops 147062784 | bytes 3719168 | tf_op jit(solution)/shard_map/while/body/eval_jaxpr/hts,shp->thp/dot_general | solution.py:178
  245.0 2.8 %multiply_reduce_fusion = (f32[512]{0:T(512)S(1)}, f32[512,1024]{0,1:T(8,128)S(1)}) fusion(bf16[512,1024]{0,1:T(8,128)(2,1)} %copy.415, bf16[512,1024]{0,1:T(8,128)(2,1)S(1)} %copy-done.2, f32[1024]{0:T(1024)S(1)} %mul.842, f32[4,512,256]{1,2,0:T(8,128)} %get-tuple-element.71), kind=kLoop, calls=%fused_computation.51 | loop fusion | flops 5766656 | bytes 6297600 | tf_op jit(solution)/shard_map/reduce_sum | solution.py:208
  247.8 9.6 %all_to_all.46 = f32[4,1,512]{2,1,0:T(1,128)S(1)} all-to-all(f32[4,1,512]{2,1,0:T(1,128)S(1)} %broadcast_in_dim.337), channel_id=1, replica_groups=mesh['seq_0'=4,'seq_1'=16,'seq_2'=2,'head'=4] {'head'}, dimensions={0} | all-to-all | bytes 16384 | tf_op jit(solution)/shard_map/all_to_all | solution.py:44
  257.6 1.3 copy.417
  (210 shorter events, 32.6 us)
Async XLA Ops:
  0.0 21.1 %copy-start = (bf16[512,128]{1,0:T(8,128)(2,1)S(1)}, bf16[512,128]{1,0:T(8,128)(2,1)}, u32[]{:S(2)}) copy-start(bf16[512,128]{1,0:T(8,128)(2,1)} %param.15) | copy-start | bytes 393220
  0.0 19.7 %copy-start.19 = (f32[512,16]{0,1:T(8,128)S(1)}, f32[512,16]{0,1:T(8,128)}, u32[]{:S(2)}) copy-start(f32[512,16]{0,1:T(8,128)} %param.17) | copy-start | bytes 98308
  3.8 17.2 %copy-start.15 = (f32[512,16]{0,1:T(8,128)}, f32[512,16]{0,1:T(8,128)S(1)}, u32[]{:S(2)}) copy-start(f32[512,16]{0,1:T(8,128)S(1)} %bitcast_bitcast_fusion) | copy-start | bytes 98308
  5.3 16.3 %all-to-all-start.1 = ((f32[4,1,1,16]{3,2,1,0:T(1,128)}), f32[4,1,1,16]{3,2,1,0:T(1,128)S(1)}, u32[]{:S(2)}, u32[]{:S(2)}) async-start(f32[4,1,1,16]{3,2,1,0:T(1,128)} %stack.9), calls=%async_computation.1 | async-start | bytes 4096 | tf_op jit(solution)/shard_map/all_to_all | solution.py:18
  17.4 47.9 %copy-start.22 = (pred[128]{0:T(512)(128)(4,1)}, pred[128]{0:T(512)(128)(4,1)S(1)}, u32[]{:S(2)}) copy-start(pred[128]{0:T(512)(128)(4,1)S(1)} %get-tuple-element.250) | copy-start | bytes 388
  17.4 47.9 %copy-start.24 = (pred[128]{0:T(512)(128)(4,1)}, pred[128]{0:T(512)(128)(4,1)S(1)}, u32[]{:S(2)}) copy-start(pred[128]{0:T(512)(128)(4,1)S(1)} %get-tuple-element.251) | copy-start | bytes 388
  18.9 2.6 %copy-start.1 = (bf16[512,1024]{0,1:T(8,128)(2,1)}, bf16[512,1024]{0,1:T(8,128)(2,1)S(1)}, u32[]{:S(2)}) copy-start(bf16[512,1024]{0,1:T(8,128)(2,1)S(1)} %copy.352) | copy-start | bytes 3145732
  21.6 43.8 %copy-start.26 = (pred[128]{0:T(512)(128)(4,1)}, pred[128]{0:T(512)(128)(4,1)S(1)}, u32[]{:S(2)}) copy-start(pred[128]{0:T(512)(128)(4,1)S(1)} %get-tuple-element.252) | copy-start | bytes 388
  21.6 43.8 %copy-start.28 = (pred[128]{0:T(512)(128)(4,1)}, pred[128]{0:T(512)(128)(4,1)S(1)}, u32[]{:S(2)}) copy-start(pred[128]{0:T(512)(128)(4,1)S(1)} %get-tuple-element.253) | copy-start | bytes 388
  22.2 23.6 %all-to-all-start.2 = ((f32[16,4,1,16]{3,1,2,0:T(4,128)}), f32[16,4,1,16]{3,1,2,0:T(4,128)S(1)}, u32[]{:S(2)}, u32[]{:S(2)}) async-start(f32[16,4,1,16]{3,1,2,0:T(4,128)} %stack.10), calls=%async_computation.2 | async-start | bytes 65536 | tf_op jit(solution)/shard_map/all_to_all | solution.py:18
  49.6 30.9 %all-to-all-start = ((bf16[128,2,512]{2,1,0:T(2,128)(2,1)}), bf16[128,2,512]{2,1,0:T(2,128)(2,1)S(1)}, u32[]{:S(2)}, u32[]{:S(2)}) async-start(bf16[128,2,512]{2,1,0:T(2,128)(2,1)} %reshape.1267), calls=%async_computation | async-start | bytes 524288 | tf_op jit(solution)/shard_map/all_to_all | solution.py:120
  58.2 23.1 %copy-start.30 = (pred[128]{0:T(512)(128)(4,1)}, pred[128]{0:T(512)(128)(4,1)S(1)}, u32[]{:S(2)}) copy-start(pred[128]{0:T(512)(128)(4,1)S(1)} %get-tuple-element.254) | copy-start | bytes 388
  58.2 23.1 %copy-start.32 = (pred[128]{0:T(512)(128)(4,1)}, pred[128]{0:T(512)(128)(4,1)S(1)}, u32[]{:S(2)}) copy-start(pred[128]{0:T(512)(128)(4,1)S(1)} %get-tuple-element.255) | copy-start | bytes 388
  61.2 25.3 %copy-start.4 = (f32[128,8]{1,0:T(8,128)}, f32[128,8]{1,0:T(8,128)S(1)}, u32[]{:S(2)}) copy-start(f32[128,8]{1,0:T(8,128)S(1)} %copy.378) | copy-start | bytes 12292
  61.2 25.3 %copy-start.5 = (f32[16,2,4,8]{3,2,1,0:T(4,128)}, f32[16,2,4,8]{3,2,1,0:T(4,128)S(1)}, u32[]{:S(2)}) copy-start(f32[16,2,4,8]{3,2,1,0:T(4,128)S(1)} %rev.44) | copy-start | bytes 12292
  61.5 25.0 %copy-start.7 = (f32[128,8]{1,0:T(8,128)}, f32[128,8]{1,0:T(8,128)S(1)}, u32[]{:S(2)}) copy-start(f32[128,8]{1,0:T(8,128)S(1)} %copy.432) | copy-start | bytes 12292
  61.8 24.7 %copy-start.8 = (f32[8,2,8,8]{3,2,1,0:T(8,128)}, f32[8,2,8,8]{3,2,1,0:T(8,128)S(1)}, u32[]{:S(2)}) copy-start(f32[8,2,8,8]{3,2,1,0:T(8,128)S(1)} %copy.433) | copy-start | bytes 12292
  98.1 8.6 %copy-start.33 = (pred[128]{0:T(512)(128)(4,1)S(1)}, pred[128]{0:T(512)(128)(4,1)}, u32[]{:S(2)}) copy-start(pred[128]{0:T(512)(128)(4,1)} %copy-done.32) | copy-start | bytes 388
  98.1 9.5 %copy-start.31 = (pred[128]{0:T(512)(128)(4,1)S(1)}, pred[128]{0:T(512)(128)(4,1)}, u32[]{:S(2)}) copy-start(pred[128]{0:T(512)(128)(4,1)} %copy-done.30) | copy-start | bytes 388
  104.6 4.9 %copy-start.14 = (f32[128,8]{1,0:T(8,128)S(1)}, f32[128,8]{1,0:T(8,128)}, u32[]{:S(2)}) copy-start(f32[128,8]{1,0:T(8,128)} %copy.370) | copy-start | bytes 12292
  104.6 4.9 %copy-start.29 = (pred[128]{0:T(512)(128)(4,1)S(1)}, pred[128]{0:T(512)(128)(4,1)}, u32[]{:S(2)}) copy-start(pred[128]{0:T(512)(128)(4,1)} %copy-done.28) | copy-start | bytes 388
  104.7 6.0 %copy-start.13 = (f32[128,8]{1,0:T(8,128)S(1)}, f32[128,8]{1,0:T(8,128)}, u32[]{:S(2)}) copy-start(f32[128,8]{1,0:T(8,128)} %copy.380) | copy-start | bytes 12292
  104.7 6.0 %copy-start.27 = (pred[128]{0:T(512)(128)(4,1)S(1)}, pred[128]{0:T(512)(128)(4,1)}, u32[]{:S(2)}) copy-start(pred[128]{0:T(512)(128)(4,1)} %copy-done.26) | copy-start | bytes 388
  104.7 7.0 %copy-start.12 = (f32[128,8]{1,0:T(8,128)S(1)}, f32[128,8]{1,0:T(8,128)}, u32[]{:S(2)}) copy-start(f32[128,8]{1,0:T(8,128)} %copy.388) | copy-start | bytes 12292
  104.7 7.0 %copy-start.25 = (pred[128]{0:T(512)(128)(4,1)S(1)}, pred[128]{0:T(512)(128)(4,1)}, u32[]{:S(2)}) copy-start(pred[128]{0:T(512)(128)(4,1)} %copy-done.24) | copy-start | bytes 388
  106.6 6.2 %copy-start.3 = (f32[2,2,32,8,128]{4,3,2,1,0:T(8,128)S(1)}, f32[2,2,32,8,128]{4,3,2,1,0:T(8,128)}, u32[]{:S(2)}) copy-start(f32[2,2,32,8,128]{4,3,2,1,0:T(8,128)} %rev.49) | copy-start | bytes 1572868
  106.6 6.2 %copy-start.11 = (f32[128,8]{1,0:T(8,128)S(1)}, f32[128,8]{1,0:T(8,128)}, u32[]{:S(2)}) copy-start(f32[128,8]{1,0:T(8,128)} %copy.394) | copy-start | bytes 12292
  106.6 6.2 %copy-start.23 = (pred[128]{0:T(512)(128)(4,1)S(1)}, pred[128]{0:T(512)(128)(4,1)}, u32[]{:S(2)}) copy-start(pred[128]{0:T(512)(128)(4,1)} %copy-done.22) | copy-start | bytes 388
  107.6 6.3 %copy-start.6 = (f32[1,2,64,8,128]{4,3,2,1,0:T(8,128)S(1)}, f32[1,2,64,8,128]{4,3,2,1,0:T(8,128)}, u32[]{:S(2)}) copy-start(f32[1,2,64,8,128]{4,3,2,1,0:T(8,128)} %rev.51) | copy-start | bytes 1572868
  107.6 6.3 %copy-start.10 = (f32[128,8]{1,0:T(8,128)S(1)}, f32[128,8]{1,0:T(8,128)}, u32[]{:S(2)}) copy-start(f32[128,8]{1,0:T(8,128)} %copy.402) | copy-start | bytes 12292
  107.6 6.3 %copy-start.34 = (pred[128]{0:T(512)(128)(4,1)S(1)}, pred[128]{0:T(512)(128)(4,1)}, u32[]{:S(2)}) copy-start(pred[128]{0:T(512)(128)(4,1)} %and_compare_fusion.21) | copy-start | bytes 388
  113.9 8.4 %copy-start.16 = (f32[512,16]{0,1:T(8,128)S(1)}, f32[512,16]{0,1:T(8,128)}, u32[]{:S(2)}) copy-start(f32[512,16]{0,1:T(8,128)} %copy-done.15) | copy-start | bytes 98308
  113.9 8.5 %copy-start.17 = (f32[512,16]{0,1:T(8,128)S(1)}, f32[512,16]{0,1:T(8,128)}, u32[]{:S(2)}) copy-start(f32[512,16]{0,1:T(8,128)} %get-tuple-element.246) | copy-start | bytes 98308
  115.0 7.4 %copy-start.18 = (f32[16,16,11]{1,0,2:T(8,128)S(1)}, f32[16,16,11]{1,0,2:T(8,128)}, u32[]{:S(2)}) copy-start(f32[16,16,11]{1,0,2:T(8,128)} %param.21) | copy-start | bytes 33796
  115.0 7.9 %copy-start.21 = (s32[512]{0:T(512)S(1)}, s32[512]{0:T(512)}, u32[]{:S(2)}) copy-start(s32[512]{0:T(512)} %param.22) | copy-start | bytes 6148
  115.0 8.6 %copy-start.9 = (bf16[512,1024]{1,0:T(8,128)(2,1)S(1)}, bf16[512,1024]{1,0:T(8,128)(2,1)}, u32[]{:S(2)}) copy-start(bf16[512,1024]{1,0:T(8,128)(2,1)} %param.14) | copy-start | bytes 3145732
  115.0 95.5 %all-to-all-start.4 = ((bf16[128,7,8,128]{3,2,1,0:T(8,128)(2,1)}), bf16[128,7,8,128]{3,2,1,0:T(8,128)(2,1)S(1)}, u32[]{:S(2)}, u32[]{:S(2)}) async-start(bf16[128,7,8,128]{3,2,1,0:T(8,128)(2,1)} %fusion.38), calls=%async_computation.4 | async-start | bytes 3670016 | tf_op jit(solution)/shard_map/all_to_all | solution.py:154
  122.4 2.5 copy-start.35
  212.1 32.9 %copy-start.2 = (bf16[512,1024]{0,1:T(8,128)(2,1)S(1)}, bf16[512,1024]{0,1:T(8,128)(2,1)}, u32[]{:S(2)}) copy-start(bf16[512,1024]{0,1:T(8,128)(2,1)} %copy-done.1) | copy-start | bytes 3145732
  245.0 12.4 %copy-start.20 = (f32[1024]{0:T(1024)S(1)}, f32[1024]{0:T(1024)}, u32[]{:S(2)}) copy-start(f32[1024]{0:T(1024)} %param.20) | copy-start | bytes 12292
